TPU v7x, 32 devices: a whole 2x2x4 slice. The times are simulated.
32 devices in a mesh: seq: 8 (over z, x), head: 4 (over y, core).
Axes of the slice: x: 2, y: 2, z: 4, core: 2. Of those that a mesh axis runs over, the one named last changes fastest.
Arguments:
- context: bfloat16 [4, 4096, 1024], P('head', 'seq'), may hold values from -6 to 6
- latents: bfloat16 [4, 1024, 1024], P('head'), may hold values from -6 to 6
- offsets: int32 [4], P('head'), may hold values from 0 to 3072
- query_gain: float32 [1024], replicated, may hold values from 0.1 to 1.9
- key_gain: float32 [1024], replicated, may hold values from 0.1 to 1.9
- layer_gain: float32 [2, 1024], replicated, may hold values from 0.1 to 1.9
- cross_query: bfloat16 [1024, 1024], P(('seq', 'head')), may hold values from -0.25 to 0.25
- cross_key: bfloat16 [1024, 1024], P(('seq', 'head')), may hold values from -0.25 to 0.25
- cross_value: bfloat16 [1024, 1024], P(('seq', 'head')), may hold values from -0.1875 to 0.1875
- cross_out: bfloat16 [1024, 1024], P(('seq', 'head')), may hold values from -0.1875 to 0.1875
- layer_qkv: bfloat16 [2, 1024, 3072], P(None, ('seq', 'head')), may hold values from -0.25 to 0.25
- layer_out: bfloat16 [2, 1024, 1024], P(None, ('seq', 'head')), may hold values from -0.1875 to 0.1875
Outputs:
- latent_out: bfloat16 [4, 1024, 1024], P('head', 'seq')
Inputs may be any that keep to these rules, and one draw needn't show every extreme that they name: Latent i of row b stands at context position offsets[b] + i.
All inputs are finite; a program needn't handle non-finite values.
Results may differ from a plain program's by a relative error of at most 0.013.
Values may be sent and summed in bfloat16 or wider, within the bound.
No kernel may reach another device: no remote copies, remote signals or barrier semaphores. Data moves between devices by JAX's collectives and lax.ppermute only.
A program may use at most 128 MiB of HBM per device.

v0:
```python
import jax
import jax.numpy as jnp
from jax import lax
from jax.sharding import PartitionSpec as P

H = 16
EPSILON = 1e-06
NEGATIVE = -1e30


def rms_norm(value_matrix, gain):
    value_matrix = value_matrix.astype(jnp.float32)
    scale = lax.rsqrt(jnp.mean(value_matrix * value_matrix, axis=-1, keepdims=True) + EPSILON)
    return (value_matrix * scale * gain).astype(jnp.bfloat16)


def project(left, weight):
    return jnp.einsum("...k,kn->...n", left, weight, preferred_element_type=jnp.float32)


def block_scores(query_row_block, key_rows, query_pos, key_base, start, key_span, scale):
    key_tile = lax.dynamic_slice_in_dim(key_rows, start, key_span, 0)
    score_matrix = (
        jnp.einsum("oqi,cqi->qoc", query_row_block, key_tile, preferred_element_type=jnp.float32)
        * scale
    )
    key_pos = key_base + start + jnp.arange(key_span, dtype=jnp.int32)
    valid = key_pos[None, None, :] <= query_pos[None, :, None]
    return (jnp.where(valid, score_matrix, NEGATIVE), valid)


def causal_top(query_row_block, key_rows, query_pos, key_base, key_span, scale):

    def advance(index, best):
        start = index * key_span

        def compute(kept):
            score_matrix, valid = block_scores(
                query_row_block, key_rows, query_pos, key_base, start, key_span, scale
            )
            return jnp.maximum(kept, jnp.max(score_matrix, axis=2))

        result = compute(best)
        return result

    initial = jnp.full((query_row_block.shape[1], query_row_block.shape[0]), NEGATIVE, jnp.float32)
    return lax.fori_loop(0, key_rows.shape[0] // key_span, advance, initial)


def causal_sums(
    query_row_block, key_rows, value_rows, row_top, query_pos, key_base, key_span, scale
):

    def advance(index, carry):
        start = index * key_span

        def compute(kept):
            numerator_sum, denom = kept
            score_matrix, valid = block_scores(
                query_row_block, key_rows, query_pos, key_base, start, key_span, scale
            )
            probability_rows = jnp.where(
                valid, jnp.exp(score_matrix - row_top[:, :, None]), 0.0
            ).astype(jnp.bfloat16)
            value_tile = lax.dynamic_slice_in_dim(value_rows, start, key_span, 0)
            numerator_sum = numerator_sum + jnp.einsum(
                "ycv,vys->cys", probability_rows, value_tile, preferred_element_type=jnp.float32
            )
            denom = denom + jnp.transpose(jnp.sum(probability_rows.astype(jnp.float32), axis=2))
            return (numerator_sum, denom)

        result = compute(carry)
        return result

    count, heads, head_width = query_row_block.shape
    initial = (
        jnp.zeros((count, heads, head_width), jnp.float32),
        jnp.zeros((count, heads), jnp.float32),
    )
    return lax.fori_loop(0, key_rows.shape[0] // key_span, advance, initial)


def latent_attention(piece):
    count = piece.shape[1]
    head_width = piece.shape[-1]
    query_matrix = piece[:, :, 0]
    key_matrix = piece[:, :, 1]
    value_matrix = piece[:, :, 2]
    score_matrix = jnp.einsum(
        "bmhd,bkhd->bhmk", query_matrix, key_matrix, preferred_element_type=jnp.float32
    ) * head_width ** (-0.5)
    positions = jnp.arange(count, dtype=jnp.int32)
    valid = positions[None, :] <= positions[:, None]
    score_matrix = jnp.where(valid, score_matrix, NEGATIVE)
    row_top = jnp.max(score_matrix, axis=3, keepdims=True)
    probability_rows = jnp.where(valid, jnp.exp(score_matrix - row_top), 0.0).astype(jnp.bfloat16)
    denom = jnp.sum(probability_rows.astype(jnp.float32), axis=3)
    numerator_sum = jnp.einsum(
        "bhmk,bkhd->bmhd", probability_rows, value_matrix, preferred_element_type=jnp.float32
    )
    return (numerator_sum / jnp.transpose(denom, (0, 2, 1))[:, :, :, None]).astype(jnp.bfloat16)


def per_device(
    context,
    latents,
    offsets,
    query_gain,
    key_gain,
    layer_gain,
    cross_query,
    cross_key,
    cross_value,
    cross_out,
    layer_qkv,
    layer_out,
):
    batch, ctx_len, width = context.shape
    latent_count = latents.shape[1]
    heads = H
    head_width = width // heads
    groups = lax.axis_size("seq")
    local_rows = latent_count // groups
    group_heads = heads // groups
    seq_index = lax.axis_index("seq")
    scale = head_width ** (-0.5)
    gathered = (
        lax.all_gather(cross_query, ("seq", "head"), axis=0, tiled=True),
        lax.all_gather(cross_key, ("seq", "head"), axis=0, tiled=True),
        lax.all_gather(cross_value, ("seq", "head"), axis=0, tiled=True),
        lax.all_gather(cross_out, ("seq", "head"), axis=0, tiled=True),
        lax.all_gather(layer_qkv, ("seq", "head"), axis=1, tiled=True),
        lax.all_gather(layer_out, ("seq", "head"), axis=1, tiled=True),
    )
    normed_latents = rms_norm(latents, query_gain)
    query_matrix = project(normed_latents, gathered[0])
    query_matrix = query_matrix.astype(jnp.bfloat16)
    normed_context = rms_norm(context, key_gain)
    key_matrix = project(normed_context, gathered[1])
    value_matrix = project(normed_context, gathered[2])
    key_matrix = key_matrix.astype(jnp.bfloat16).reshape(batch, ctx_len, heads, head_width)
    value_matrix = value_matrix.astype(jnp.bfloat16).reshape(batch, ctx_len, heads, head_width)
    query_head_rows = query_matrix.reshape(batch, latent_count, heads, head_width)
    query_pos = offsets[:, None] + jnp.arange(latent_count, dtype=jnp.int32)[None, :]
    key_groups, value_groups = (
        lax.all_to_all(key_matrix, "seq", split_axis=2, concat_axis=1, tiled=True),
        lax.all_to_all(value_matrix, "seq", split_axis=2, concat_axis=1, tiled=True),
    )
    query_groups = lax.dynamic_slice_in_dim(
        query_head_rows, seq_index * group_heads, group_heads, 2
    )
    total_len = key_groups.shape[1]
    key_span = max(min(total_len, 512), total_len // 16)
    row_top = causal_top(query_groups[0], key_groups[0], query_pos[0], 0, key_span, scale)
    numerator_sum, denom = causal_sums(
        query_groups[0], key_groups[0], value_groups[0], row_top, query_pos[0], 0, key_span, scale
    )
    results = [(numerator_sum / denom[:, :, None]).astype(jnp.bfloat16)]
    attended = lax.all_to_all(
        jnp.stack(results), "seq", split_axis=1, concat_axis=2, tiled=True
    ).reshape(batch, local_rows, width)
    latents_own = lax.dynamic_slice_in_dim(latents, seq_index * local_rows, local_rows, 1)
    update = project(attended, gathered[3])
    hidden = (latents_own.astype(jnp.float32) + update).astype(jnp.bfloat16)
    for layer in range(layer_qkv.shape[0]):
        normed = rms_norm(hidden, layer_gain[layer])
        qkv = project(normed, gathered[4][layer])
        grouped = qkv.astype(jnp.bfloat16).reshape(batch, local_rows, 3, heads, head_width)
        mixed = latent_attention(
            lax.all_to_all(grouped, "seq", split_axis=3, concat_axis=1, tiled=True)
        )
        merged = lax.all_to_all(mixed, "seq", split_axis=1, concat_axis=2, tiled=True).reshape(
            batch, local_rows, width
        )
        update = project(merged, gathered[5][layer])
        hidden = (hidden.astype(jnp.float32) + update).astype(jnp.bfloat16)
    return hidden


def solution(mesh):
    return jax.shard_map(
        per_device,
        mesh=mesh,
        in_specs=(
            P("head", "seq", None),
            P("head", None, None),
            P("head"),
            P(),
            P(),
            P(),
            P(("seq", "head"), None),
            P(("seq", "head"), None),
            P(("seq", "head"), None),
            P(("seq", "head"), None),
            P(None, ("seq", "head"), None),
            P(None, ("seq", "head"), None),
        ),
        out_specs=P("head", "seq", None),
        check_vma=False,
    )
```

profile of v0, /device:TPU:0, one launch (start us, length us, event | category | flops | bytes accessed | tf_op | source)
XLA Modules:
  0.0 485.0 jit_solution(4928080488201104973)
XLA Ops:
  6.5 0.7 all-gather.9.cloned.1.call-update
  7.3 0.7 all-gather.7.cloned.1.call-update
  9.9 1.5 fusion.33
  11.4 57.8 %all-gather.9.cloned.1.call-done = bf16[1024,1024]{1,0:T(8,128)(2,1)} async-done(((bf16[32,1024]{1,0:T(8,128)(2,1)}), bf16[1024,1024]{1,0:T(8,128)(2,1)}) %all-gather.9.cloned.1.call-update) | async-done | bytes 2097168 | tf_op jit(solution)/shard_map/all_gather | solution.py:129
  69.2 3.2 convolution_convert_fusion
  72.4 1.3 copy.73
  73.8 4.3 all-to-all-start.1
  78.7 2.1 fusion.22
  80.8 51.9 %all-gather.7.cloned.1.call-done = bf16[1024,1024]{1,0:T(8,128)(2,1)} async-done(((bf16[32,1024]{1,0:T(8,128)(2,1)}), bf16[1024,1024]{1,0:T(8,128)(2,1)}) %all-gather.7.cloned.1.call-update) | async-done | bytes 2097168 | tf_op jit(solution)/shard_map/all_gather | solution.py:130
  132.7 3.9 convolution_convert_fusion.1
  136.6 2.3 copy.70
  138.9 51.8 %all-gather.11.cloned.1.call-done = bf16[1024,1024]{1,0:T(8,128)(2,1)} async-done(((bf16[32,1024]{1,0:T(8,128)(2,1)}), bf16[1024,1024]{1,0:T(8,128)(2,1)}) %all-gather.11.cloned.1.call-update) | async-done | bytes 2097168 | tf_op jit(solution)/shard_map/all_gather | solution.py:128
  190.7 4.8 fusion.43
  195.5 4.3 all-to-all-start
  199.9 1.6 copy.75
  201.4 1.6 squeeze.30
  203.0 16.9 %while.30 = (s32[]{:T(128)}, f32[2,1024]{1,0:T(2,128)S(1)}, bf16[4096,2,64]{0,2,1:T(8,128)(2,1)S(1)}, bf16[1024,2,64]{0,2,1:T(8,128)(2,1)S(1)}, s32[]{:T(128)}, ...) while((s32[]{:T(128)}, f32[2,1024]{1,0:T(2,128)S(1)}, bf16[4096,2,64]{0,2,1:T(8,128)(2,1)S(1)}, ...), condition=%wide.region_4.5_spmd.clone, body=%wide.region_2.4_spmd.clone.sunk | while | flops 137891328 | bytes 1487009 | solution.py:47
  204.0 1.0 fusion.103
  206.1 1.0 fusion.103
  208.3 1.0 fusion.103
  210.4 1.0 fusion.103
  212.5 1.0 fusion.103
  214.6 1.0 fusion.103
  216.7 1.0 fusion.103
  218.8 1.0 fusion.103
  219.9 8.5 %all-to-all-done = bf16[1,512,16,64]{1,3,0,2:T(8,128)(2,1)S(1)} async-done(((bf16[1,512,16,64]{1,3,0,2:T(8,128)(2,1)}), bf16[1,512,16,64]{1,3,0,2:T(8,128)(2,1)S(1)}, u32[]{:S(2)}, u32[]{:S(2)}) %all-to-all-start) | async-done | bytes 1048608 | tf_op jit(solution)/shard_map/all_to_all | solution.py:147
  228.9 1.3 squeeze.14
  230.2 40.6 %while.31 = (s32[]{:T(128)}, f32[1024,2,64]{0,2,1:T(8,128)S(1)}, f32[1024,2]{0,1:T(2,128)S(1)}, bf16[4096,2,64]{0,2,1:T(8,128)(2,1)}, bf16[4096,2,64]{0,2,1:T(8,...) while((s32[]{:T(128)}, f32[1024,2,64]{0,2,1:T(8,128)S(1)}, ...), condition=%wide.region_7.8_spmd.clone, body=%wide.region_5.7_spmd.clone.sunk | while | flops 276565504 | bytes 6869182 | solution.py:80
  231.3 2.5 convert_reduce_fusion.4
  233.8 1.4 fusion.107
  236.3 2.5 convert_reduce_fusion.4
  238.9 1.5 fusion.107
  241.5 2.5 convert_reduce_fusion.4
  244.0 1.4 fusion.107
  246.5 2.5 convert_reduce_fusion.4
  249.1 1.4 fusion.107
  251.6 2.5 convert_reduce_fusion.4
  254.1 1.4 fusion.107
  256.7 2.5 convert_reduce_fusion.4
  259.2 1.4 fusion.107
  261.7 2.5 convert_reduce_fusion.4
  264.3 1.5 fusion.107
  266.8 2.5 convert_reduce_fusion.4
  269.3 1.4 fusion.107
  271.6 1.1 reshape.307
  272.7 3.5 all-to-all-start.2
  276.3 9.1 %all-to-all-done.2 = bf16[8,2,8192]{2,1,0:T(2,128)(2,1)S(1)} async-done(((bf16[8,2,8192]{2,1,0:T(2,128)(2,1)}), bf16[8,2,8192]{2,1,0:T(2,128)(2,1)S(1)}, u32[]{:S(2)}, u32[]{:S(2)}) %all-to-all-start.2) | async-done | bytes 262176 | tf_op jit(solution)/shard_map/all_to_all | solution.py:159
  286.1 2.1 multiply_reduce_fusion.1
  288.3 64.0 %all-gather.15.cloned.1.call-done = bf16[2,1024,3072]{2,1,0:T(8,128)(2,1)} async-done(((bf16[2,32,3072]{2,1,0:T(8,128)(2,1)}), bf16[2,1024,3072]{2,1,0:T(8,128)(2,1)}) %all-gather.15.cloned.1.call-update) | async-done | bytes 12582928 | tf_op jit(solution)/shard_map/all_gather | solution.py:132
  352.3 3.8 fusion.31
  356.5 0.9 copy.82
  357.4 4.0 all-to-all-start.3
  361.8 23.0 %all-to-all-done.3 = bf16[1,128,3,16,64]{1,4,2,0,3:T(8,128)(2,1)S(1)} async-done(((bf16[1,128,3,16,64]{1,4,2,0,3:T(8,128)(2,1)}), bf16[1,128,3,16,64]{1,4,2,0,3:T(8,128)(2,1)S(1)}, u32[]{:S(2)}, u32[]{:S(2)}) %all-to-all-start.3) | async-done | bytes 786464 | tf_op jit(solution)/shard_map/all_to_all | solution.py:170
  385.6 6.0 %convert_reduce_fusion.2 = (f32[2,1024]{1,0:T(2,128)S(1)}, bf16[2,1024,1024]{1,2,0:T(8,128)(2,1)}) fusion(pred[1024,1024]{0,1:T(8,128)(4,1)S(1)} %iota_compare_fusion, bf16[1,1024,3,2,64]{1,4,3,2,0:T(8,128)(2,1)S(1)} %all_to_all.93), kind=kOutput, calls=%fused_computation.31 | convolution fusion | flops 283116544 | bytes 6823936 | tf_op jit(solution)/shard_map/sub | solution.py:96
  391.6 3.0 fusion.57
  395.5 18.1 %all_to_all.111 = bf16[8,2,8192]{2,1,0:T(2,128)(2,1)S(1)} all-to-all(bf16[8,2,8192]{2,1,0:T(2,128)(2,1)S(1)} %reshape.309), channel_id=1, replica_groups=mesh['seq'=8,'head'=4] {'seq'}, dimensions={0} | all-to-all | bytes 524288 | tf_op jit(solution)/shard_map/all_to_all | solution.py:172
  414.2 6.9 %all-gather.17.cloned.1.call-done = bf16[2,1024,1024]{2,1,0:T(8,128)(2,1)} async-done(((bf16[2,32,1024]{2,1,0:T(8,128)(2,1)}), bf16[2,1024,1024]{2,1,0:T(8,128)(2,1)}) %all-gather.17.cloned.1.call-update) | async-done | bytes 4194320 | tf_op jit(solution)/shard_map/all_gather | solution.py:133
  421.1 2.1 multiply_reduce_fusion
  423.3 3.8 fusion.32
  427.6 24.1 %all_to_all.112 = bf16[1,128,3,16,64]{1,4,2,0,3:T(8,128)(2,1)S(1)} all-to-all(bf16[1,128,3,16,64]{1,4,2,0,3:T(8,128)(2,1)S(1)} %copy.89), channel_id=1, replica_groups=mesh['seq'=8,'head'=4] {'seq'}, dimensions={3} | all-to-all | bytes 1572864 | tf_op jit(solution)/shard_map/all_to_all | solution.py:170
  452.5 6.0 %convert_reduce_fusion.1 = (f32[2,1024]{1,0:T(2,128)S(1)}, bf16[2,1024,1024]{1,2,0:T(8,128)(2,1)}) fusion(pred[1024,1024]{0,1:T(8,128)(4,1)S(1)} %iota_compare_fusion, bf16[1,1024,3,2,64]{1,4,3,2,0:T(8,128)(2,1)S(1)} %all_to_all.100), kind=kOutput, calls=%fused_computation.28 | convolution fusion | flops 283116544 | bytes 6823936 | tf_op jit(solution)/shard_map/sub | solution.py:96
  458.5 3.0 fusion.59
  462.4 12.3 %all_to_all.113 = bf16[8,2,8192]{2,1,0:T(2,128)(2,1)S(1)} all-to-all(bf16[8,2,8192]{2,1,0:T(2,128)(2,1)S(1)} %reshape.311), channel_id=1, replica_groups=mesh['seq'=8,'head'=4] {'seq'}, dimensions={0} | all-to-all | bytes 524288 | tf_op jit(solution)/shard_map/all_to_all | solution.py:172
  475.4 2.8 fusion.55
  (120 shorter events, 26.9 us)
Async XLA Ops:
  6.5 62.7 %all-gather.9.cloned.1.call-start = ((), (), s32[]{:S(2)}) async-start(), calls=%async_computation.8 | async-start | bytes 2162688 | tf_op jit(solution)/shard_map/all_gather | solution.py:129
  7.3 125.4 %all-gather.7.cloned.1.call-start = ((), (), s32[]{:S(2)}) async-start(), calls=%async_computation.7 | async-start | bytes 2162688 | tf_op jit(solution)/shard_map/all_gather | solution.py:130
  8.0 182.7 %all-gather.11.cloned.1.call-start = ((), (), s32[]{:S(2)}) async-start(), calls=%async_computation.9 | async-start | bytes 2162688 | tf_op jit(solution)/shard_map/all_gather | solution.py:128
  8.7 277.4 %all-gather.13.cloned.1.call-start = ((), (), s32[]{:S(2)}) async-start(), calls=%async_computation.10 | async-start | bytes 2162688 | tf_op jit(solution)/shard_map/all_gather | solution.py:131
  9.3 343.0 %all-gather.15.cloned.1.call-start = ((), (), s32[]{:S(2)}) async-start(), calls=%async_computation.11 | async-start | bytes 12976128 | tf_op jit(solution)/shard_map/all_gather | solution.py:132
  72.4 60.3 %copy-start = (bf16[1,512,1024]{2,1,0:T(8,128)(2,1)S(1)}, bf16[1,512,1024]{2,1,0:T(8,128)(2,1)}, u32[]{:S(2)}) copy-start(bf16[1,512,1024]{2,1,0:T(8,128)(2,1)} %param.16) | copy-start | bytes 3145732
  72.4 60.2 %copy-start.3 = (f32[1024]{0:T(1024)S(1)}, f32[1024]{0:T(1024)}, u32[]{:S(2)}) copy-start(f32[1024]{0:T(1024)} %param.20) | copy-start | bytes 12292
  73.8 121.7 %all-to-all-start.1 = ((bf16[1,512,16,64]{1,3,0,2:T(8,128)(2,1)}), bf16[1,512,16,64]{1,3,0,2:T(8,128)(2,1)S(1)}, u32[]{:S(2)}, u32[]{:S(2)}) async-start(bf16[1,512,16,64]{1,3,0,2:T(8,128)(2,1)} %bitcast.6), calls=%async_computation.1 | async-start | bytes 2097152 | tf_op jit(solution)/shard_map/all_to_all | solution.py:146
  78.1 343.1 %all-gather.17.cloned.1.call-start = ((), (), s32[]{:S(2)}) async-start(), calls=%async_computation.12 | async-start | bytes 4325376 | tf_op jit(solution)/shard_map/all_gather | solution.py:133
  80.8 109.9 %copy-start.4 = (f32[1024]{0:T(1024)S(1)}, f32[1024]{0:T(1024)}, u32[]{:S(2)}) copy-start(f32[1024]{0:T(1024)} %param.19) | copy-start | bytes 12292
  195.5 32.8 %all-to-all-start = ((bf16[1,512,16,64]{1,3,0,2:T(8,128)(2,1)}), bf16[1,512,16,64]{1,3,0,2:T(8,128)(2,1)S(1)}, u32[]{:S(2)}, u32[]{:S(2)}) async-start(bf16[1,512,16,64]{1,3,0,2:T(8,128)(2,1)} %bitcast.2), calls=%async_computation | async-start | bytes 2097152 | tf_op jit(solution)/shard_map/all_to_all | solution.py:147
  219.8 8.5 %copy-start.1 = (bf16[4096,2,64]{0,2,1:T(8,128)(2,1)}, bf16[4096,2,64]{0,2,1:T(8,128)(2,1)S(1)}, u32[]{:S(2)}) copy-start(bf16[4096,2,64]{0,2,1:T(8,128)(2,1)S(1)} %get-tuple-element.490) | copy-start | bytes 3145732
  230.2 46.0 %copy-start.2 = (f32[2,1024]{1,0:T(2,128)S(1)}, f32[2,1024]{1,0:T(2,128)}, u32[]{:S(2)}) copy-start(f32[2,1024]{1,0:T(2,128)} %param.21) | copy-start | bytes 24580
  272.7 12.7 %all-to-all-start.2 = ((bf16[8,2,8192]{2,1,0:T(2,128)(2,1)}), bf16[8,2,8192]{2,1,0:T(2,128)(2,1)S(1)}, u32[]{:S(2)}, u32[]{:S(2)}) async-start(bf16[8,2,8192]{2,1,0:T(2,128)(2,1)} %reshape.307), calls=%async_computation.2 | async-start | bytes 524288 | tf_op jit(solution)/shard_map/all_to_all | solution.py:159
  357.4 27.3 %all-to-all-start.3 = ((bf16[1,128,3,16,64]{1,4,2,0,3:T(8,128)(2,1)}), bf16[1,128,3,16,64]{1,4,2,0,3:T(8,128)(2,1)S(1)}, u32[]{:S(2)}, u32[]{:S(2)}) async-start(bf16[1,128,3,16,64]{1,4,2,0,3:T(8,128)(2,1)} %copy.82), calls=%async_computation.3 | async-start | bytes 1572864 | tf_op jit(solution)/shard_map/all_to_all | solution.py:170
Sparse Core Ops, SparseCore 0:
  10.2 58.9 all-gather.8
  72.0 60.5 all-gather.6
  135.5 55.0 all-gather.10
  193.4 61.0 all-gather.12
  257.3 94.9 all-gather.14
  355.1 66.0 all-gather.16
where the time goes:
time: 486 us; the launch traced here: 485 us
  waiting for transfers between devices  277 us (57%)
  matrix products  84.7 us (17%)
  blocking collectives  54.5 us (11%)
  other arithmetic  20.5 us (4%)
  local copies, waits for them, and re-layouts  17.5 us (4%)
  starting transfers between devices  16.4 us (3%)
  between operations  13.8 us (3%)
    all_gather x1, waiting for transfers between devices, per_device(): lax.all_gather(layer_qkv, ('seq', 'head'), axis=1, tiled=True)  64 us
    all_gather x1, waiting for transfers between devices, per_device(): lax.all_gather(cross_key, ('seq', 'head'), axis=0, tiled=True)  57.8 us
    all_gather x1, waiting for transfers between devices, per_device(): lax.all_gather(cross_value, ('seq', 'head'), axis=0, tiled=True)  51.9 us
    all_gather x1, waiting for transfers between devices, per_device(): lax.all_gather(cross_query, ('seq', 'head'), axis=0, tiled=True)  51.8 us
    all_to_all x2, blocking collectives, per_device(): lax.all_to_all(mixed, 'seq', split_axis=1, concat_axis=2, tiled=True)  30.4 us
    dot_general x16, matrix products, block_scores(): jnp.einsum('oqi,cqi->qoc', query_row_block, key_tile, preferred_element_t...  28.3 us
    dot_general x8, matrix products, project(): jnp.einsum('...k,kn->...n', left, weight, preferred_element_type=jnp.floa...  26.6 us
    all_to_all x1, blocking collectives, per_device(): lax.all_to_all(grouped, 'seq', split_axis=3, concat_axis=1, tiled=True)  24.1 us
  transfers between devices with their start and end apart: 10, of which 8 were waited for; matrix products, arithmetic and copies ran while one was open for 21% of the time, Pallas kernels for 0%

commit v1 on v0

--- a/solution.py
+++ b/solution.py
@@ -169,9 +169,10 @@
         mixed = latent_attention(
             lax.all_to_all(grouped, "seq", split_axis=3, concat_axis=1, tiled=True)
         )
-        merged = lax.all_to_all(mixed, "seq", split_axis=1, concat_axis=2, tiled=True).reshape(
-            batch, local_rows, width
-        )
+        merged = jnp.concatenate(
+            lax.all_to_all(jnp.stack(jnp.split(mixed, lax.axis_size("seq"), axis=1)), "seq", 0, 0),
+            axis=2,
+        ).reshape(batch, local_rows, width)
         update = project(merged, gathered[5][layer])
         hidden = (hidden.astype(jnp.float32) + update).astype(jnp.bfloat16)
     return hidden

time: 486 us -> 486 us (level)
  blocking collectives: 54.5 us -> 36.4 us
  waiting for transfers between devices: 277 us -> 290 us
    all_to_all x2 -> x1, blocking collectives: 30.4 us -> 12.3 us  [per_device(): lax.all_to_all(jnp.stack(jnp.split(mixed, lax.axis_size('seq'), axis=1)),...]
    all_gather x1, waiting for transfers between devices: 6.91 us -> 19.9 us  [per_device(): lax.all_gather(layer_out, ('seq', 'head'), axis=1, tiled=True)]
  transfers between devices with their start and end apart: 10 -> 11, of which waited for: 8 -> 8; matrix products, arithmetic and copies ran while one was open for 21% -> 22% of each run, Pallas kernels for 0% -> 0%
where the time goes in v1:
time: 486 us; the launch traced here: 484 us
  waiting for transfers between devices  290 us (60%)
  matrix products  83.2 us (17%)
  blocking collectives  36.4 us (7%)
  other arithmetic  20.5 us (4%)
  starting transfers between devices  20 us (4%)
  local copies, waits for them, and re-layouts  19.8 us (4%)
  between operations  13.8 us (3%)
    all_gather x1, waiting for transfers between devices, per_device(): lax.all_gather(layer_qkv, ('seq', 'head'), axis=1, tiled=True)  64.2 us
    all_gather x1, waiting for transfers between devices, per_device(): lax.all_gather(cross_key, ('seq', 'head'), axis=0, tiled=True)  57.8 us
    all_gather x1, waiting for transfers between devices, per_device(): lax.all_gather(cross_value, ('seq', 'head'), axis=0, tiled=True)  51.9 us
    all_gather x1, waiting for transfers between devices, per_device(): lax.all_gather(cross_query, ('seq', 'head'), axis=0, tiled=True)  51.8 us
    dot_general x16, matrix products, block_scores(): jnp.einsum('oqi,cqi->qoc', query_row_block, key_tile, preferred_element_t...  28.4 us
    dot_general x8, matrix products, project(): jnp.einsum('...k,kn->...n', left, weight, preferred_element_type=jnp.floa...  25 us
    all_to_all x1, blocking collectives, per_device(): lax.all_to_all(grouped, 'seq', split_axis=3, concat_axis=1, tiled=True)  24.1 us
    all_to_all x1, waiting for transfers between devices, per_device(): lax.all_to_all(grouped, 'seq', split_axis=3, concat_axis=1, tiled=True)  23 us
  transfers between devices with their start and end apart: 11, of which 8 were waited for; matrix products, arithmetic and copies ran while one was open for 22% of the time, Pallas kernels for 0%

profile of v1, /device:TPU:0, one launch (start us, length us, event | category | flops | bytes accessed | tf_op | source)
XLA Modules:
  0.0 484.5 jit_solution(5945957646295921035)
XLA Ops:
  6.5 0.7 all-gather.9.cloned.1.call-update
  7.3 0.7 all-gather.7.cloned.1.call-update
  9.9 1.5 fusion.33
  11.4 57.8 %all-gather.9.cloned.1.call-done = bf16[1024,1024]{1,0:T(8,128)(2,1)} async-done(((bf16[32,1024]{1,0:T(8,128)(2,1)}), bf16[1024,1024]{1,0:T(8,128)(2,1)}) %all-gather.9.cloned.1.call-update) | async-done | bytes 2097168 | tf_op jit(solution)/shard_map/all_gather | solution.py:129
  69.2 3.2 convolution_convert_fusion
  72.4 1.3 copy.47
  73.8 4.3 all-to-all-start.1
  78.7 2.1 fusion.22
  80.8 51.9 %all-gather.7.cloned.1.call-done = bf16[1024,1024]{1,0:T(8,128)(2,1)} async-done(((bf16[32,1024]{1,0:T(8,128)(2,1)}), bf16[1024,1024]{1,0:T(8,128)(2,1)}) %all-gather.7.cloned.1.call-update) | async-done | bytes 2097168 | tf_op jit(solution)/shard_map/all_gather | solution.py:130
  132.7 3.9 convolution_convert_fusion.1
  136.6 2.3 copy.44
  138.8 51.8 %all-gather.11.cloned.1.call-done = bf16[1024,1024]{1,0:T(8,128)(2,1)} async-done(((bf16[32,1024]{1,0:T(8,128)(2,1)}), bf16[1024,1024]{1,0:T(8,128)(2,1)}) %all-gather.11.cloned.1.call-update) | async-done | bytes 2097168 | tf_op jit(solution)/shard_map/all_gather | solution.py:128
  190.7 4.8 fusion.43
  195.5 4.3 all-to-all-start
  199.8 1.6 copy.49
  201.4 1.6 squeeze.30
  203.0 16.9 %while.30 = (s32[]{:T(128)}, f32[2,1024]{1,0:T(2,128)S(1)}, bf16[4096,2,64]{0,2,1:T(8,128)(2,1)S(1)}, bf16[1024,2,64]{0,2,1:T(8,128)(2,1)S(1)}, s32[]{:T(128)}, ...) while((s32[]{:T(128)}, f32[2,1024]{1,0:T(2,128)S(1)}, bf16[4096,2,64]{0,2,1:T(8,128)(2,1)S(1)}, ...), condition=%wide.region_4.5_spmd.clone, body=%wide.region_2.4_spmd.clone.sunk | while | flops 137891328 | bytes 1487009 | solution.py:47
  204.0 1.0 fusion.103
  206.1 1.0 fusion.103
  208.2 1.0 fusion.103
  210.3 1.0 fusion.103
  212.4 1.0 fusion.103
  214.6 1.0 fusion.103
  216.7 1.0 fusion.103
  218.8 1.0 fusion.103
  219.8 8.5 %all-to-all-done = bf16[1,512,16,64]{1,3,0,2:T(8,128)(2,1)S(1)} async-done(((bf16[1,512,16,64]{1,3,0,2:T(8,128)(2,1)}), bf16[1,512,16,64]{1,3,0,2:T(8,128)(2,1)S(1)}, u32[]{:S(2)}, u32[]{:S(2)}) %all-to-all-start) | async-done | bytes 1048608 | tf_op jit(solution)/shard_map/all_to_all | solution.py:147
  228.9 1.3 squeeze.14
  230.2 40.6 %while.31 = (s32[]{:T(128)}, f32[1024,2,64]{0,2,1:T(8,128)S(1)}, f32[1024,2]{0,1:T(2,128)S(1)}, bf16[4096,2,64]{0,2,1:T(8,128)(2,1)}, bf16[4096,2,64]{0,2,1:T(8,...) while((s32[]{:T(128)}, f32[1024,2,64]{0,2,1:T(8,128)S(1)}, ...), condition=%wide.region_7.8_spmd.clone, body=%wide.region_5.7_spmd.clone.sunk | while | flops 276565504 | bytes 6869182 | solution.py:80
  231.3 2.5 convert_reduce_fusion.4
  233.8 1.4 fusion.107
  236.3 2.5 convert_reduce_fusion.4
  238.9 1.5 fusion.107
  241.5 2.5 convert_reduce_fusion.4
  244.0 1.4 fusion.107
  246.5 2.5 convert_reduce_fusion.4
  249.1 1.4 fusion.107
  251.6 2.5 convert_reduce_fusion.4
  254.1 1.4 fusion.107
  256.7 2.5 convert_reduce_fusion.4
  259.2 1.4 fusion.107
  261.7 2.5 convert_reduce_fusion.4
  264.3 1.5 fusion.107
  266.8 2.5 convert_reduce_fusion.4
  269.3 1.4 fusion.107
  271.7 1.1 reshape.311
  272.7 3.5 all-to-all-start.2
  276.3 9.1 %all-to-all-done.2 = bf16[8,2,8192]{2,1,0:T(2,128)(2,1)S(1)} async-done(((bf16[8,2,8192]{2,1,0:T(2,128)(2,1)}), bf16[8,2,8192]{2,1,0:T(2,128)(2,1)S(1)}, u32[]{:S(2)}, u32[]{:S(2)}) %all-to-all-start.2) | async-done | bytes 262176 | tf_op jit(solution)/shard_map/all_to_all | solution.py:159
  286.1 2.1 multiply_reduce_fusion.1
  288.3 64.2 %all-gather.15.cloned.1.call-done = bf16[2,1024,3072]{2,1,0:T(8,128)(2,1)} async-done(((bf16[2,32,3072]{2,1,0:T(8,128)(2,1)}), bf16[2,1024,3072]{2,1,0:T(8,128)(2,1)}) %all-gather.15.cloned.1.call-update) | async-done | bytes 12582928 | tf_op jit(solution)/shard_map/all_gather | solution.py:132
  352.5 3.8 fusion.31
  356.7 0.9 copy.56
  357.6 4.0 all-to-all-start.3
  362.0 23.0 %all-to-all-done.3 = bf16[1,128,3,16,64]{1,4,2,0,3:T(8,128)(2,1)S(1)} async-done(((bf16[1,128,3,16,64]{1,4,2,0,3:T(8,128)(2,1)}), bf16[1,128,3,16,64]{1,4,2,0,3:T(8,128)(2,1)S(1)}, u32[]{:S(2)}, u32[]{:S(2)}) %all-to-all-start.3) | async-done | bytes 786464 | tf_op jit(solution)/shard_map/all_to_all | solution.py:170
  385.8 6.0 %convert_reduce_fusion.2 = (f32[2,1024]{1,0:T(2,128)S(1)}, bf16[2,1024,1024]{1,2,0:T(8,128)(2,1)}) fusion(pred[1024,1024]{0,1:T(8,128)(4,1)S(1)} %iota_compare_fusion, bf16[1,1024,3,2,64]{1,4,3,2,0:T(8,128)(2,1)S(1)} %all_to_all.77), kind=kOutput, calls=%fused_computation.31 | convolution fusion | flops 283116544 | bytes 6823936 | tf_op jit(solution)/shard_map/sub | solution.py:96
  391.8 3.0 fusion.57
  399.9 3.6 all-to-all-start.4
  403.5 19.9 %all-gather.17.cloned.1.call-done = bf16[2,1024,1024]{2,1,0:T(8,128)(2,1)} async-done(((bf16[2,32,1024]{2,1,0:T(8,128)(2,1)}), bf16[2,1024,1024]{2,1,0:T(8,128)(2,1)}) %all-gather.17.cloned.1.call-update) | async-done | bytes 4194320 | tf_op jit(solution)/shard_map/all_gather | solution.py:133
  423.4 2.1 multiply_reduce_fusion
  425.5 3.8 fusion.32
  429.8 24.1 %all_to_all.91 = bf16[1,128,3,16,64]{1,4,2,0,3:T(8,128)(2,1)S(1)} all-to-all(bf16[1,128,3,16,64]{1,4,2,0,3:T(8,128)(2,1)S(1)} %copy.60), channel_id=1, replica_groups=mesh['seq'=8,'head'=4] {'seq'}, dimensions={3} | all-to-all | bytes 1572864 | tf_op jit(solution)/shard_map/all_to_all | solution.py:170
  454.8 6.0 %convert_reduce_fusion.1 = (f32[2,1024]{1,0:T(2,128)S(1)}, bf16[2,1024,1024]{1,2,0:T(8,128)(2,1)}) fusion(pred[1024,1024]{0,1:T(8,128)(4,1)S(1)} %iota_compare_fusion, bf16[1,1024,3,2,64]{1,4,3,2,0:T(8,128)(2,1)S(1)} %all_to_all.82), kind=kOutput, calls=%fused_computation.28 | convolution fusion | flops 283116544 | bytes 6823936 | tf_op jit(solution)/shard_map/sub | solution.py:96
  460.7 3.2 fusion.59
  464.1 12.3 %all_to_all.92 = bf16[8,1,128,2,64]{2,4,3,1,0:T(8,128)(2,1)S(1)} all-to-all(bf16[8,1,128,2,64]{2,4,3,1,0:T(8,128)(2,1)S(1)} %constant_dynamic-update-slice_fusion.8), channel_id=1, replica_groups=mesh['seq'=8,'head'=4] {'seq'}, dimensions={0} | all-to-all | bytes 524288 | tf_op jit(solution)/shard_map/all_to_all | solution.py:173
  476.4 1.2 fusion.55
  (129 shorter events, 29.1 us)
Async XLA Ops:
  6.5 62.7 %all-gather.9.cloned.1.call-start = ((), (), s32[]{:S(2)}) async-start(), calls=%async_computation.8 | async-start | bytes 2162688 | tf_op jit(solution)/shard_map/all_gather | solution.py:129
  7.3 125.4 %all-gather.7.cloned.1.call-start = ((), (), s32[]{:S(2)}) async-start(), calls=%async_computation.7 | async-start | bytes 2162688 | tf_op jit(solution)/shard_map/all_gather | solution.py:130
  8.0 182.6 %all-gather.11.cloned.1.call-start = ((), (), s32[]{:S(2)}) async-start(), calls=%async_computation.9 | async-start | bytes 2162688 | tf_op jit(solution)/shard_map/all_gather | solution.py:128
  8.7 277.3 %all-gather.13.cloned.1.call-start = ((), (), s32[]{:S(2)}) async-start(), calls=%async_computation.10 | async-start | bytes 2162688 | tf_op jit(solution)/shard_map/all_gather | solution.py:131
  9.3 343.2 %all-gather.15.cloned.1.call-start = ((), (), s32[]{:S(2)}) async-start(), calls=%async_computation.11 | async-start | bytes 12976128 | tf_op jit(solution)/shard_map/all_gather | solution.py:132
  72.4 60.2 %copy-start.1 = (bf16[1,512,1024]{2,1,0:T(8,128)(2,1)S(1)}, bf16[1,512,1024]{2,1,0:T(8,128)(2,1)}, u32[]{:S(2)}) copy-start(bf16[1,512,1024]{2,1,0:T(8,128)(2,1)} %param.16) | copy-start | bytes 3145732
  72.4 60.2 %copy-start.4 = (f32[1024]{0:T(1024)S(1)}, f32[1024]{0:T(1024)}, u32[]{:S(2)}) copy-start(f32[1024]{0:T(1024)} %param.20) | copy-start | bytes 12292
  73.8 121.7 %all-to-all-start.1 = ((bf16[1,512,16,64]{1,3,0,2:T(8,128)(2,1)}), bf16[1,512,16,64]{1,3,0,2:T(8,128)(2,1)S(1)}, u32[]{:S(2)}, u32[]{:S(2)}) async-start(bf16[1,512,16,64]{1,3,0,2:T(8,128)(2,1)} %bitcast.6), calls=%async_computation.1 | async-start | bytes 2097152 | tf_op jit(solution)/shard_map/all_to_all | solution.py:146
  78.1 345.3 %all-gather.17.cloned.1.call-start = ((), (), s32[]{:S(2)}) async-start(), calls=%async_computation.12 | async-start | bytes 4325376 | tf_op jit(solution)/shard_map/all_gather | solution.py:133
  80.8 109.9 %copy-start.5 = (f32[1024]{0:T(1024)S(1)}, f32[1024]{0:T(1024)}, u32[]{:S(2)}) copy-start(f32[1024]{0:T(1024)} %param.19) | copy-start | bytes 12292
  195.5 32.8 %all-to-all-start = ((bf16[1,512,16,64]{1,3,0,2:T(8,128)(2,1)}), bf16[1,512,16,64]{1,3,0,2:T(8,128)(2,1)S(1)}, u32[]{:S(2)}, u32[]{:S(2)}) async-start(bf16[1,512,16,64]{1,3,0,2:T(8,128)(2,1)} %bitcast.2), calls=%async_computation | async-start | bytes 2097152 | tf_op jit(solution)/shard_map/all_to_all | solution.py:147
  219.8 8.5 %copy-start.2 = (bf16[4096,2,64]{0,2,1:T(8,128)(2,1)}, bf16[4096,2,64]{0,2,1:T(8,128)(2,1)S(1)}, u32[]{:S(2)}) copy-start(bf16[4096,2,64]{0,2,1:T(8,128)(2,1)S(1)} %get-tuple-element.491) | copy-start | bytes 3145732
  230.2 46.0 %copy-start.3 = (f32[2,1024]{1,0:T(2,128)S(1)}, f32[2,1024]{1,0:T(2,128)}, u32[]{:S(2)}) copy-start(f32[2,1024]{1,0:T(2,128)} %param.21) | copy-start | bytes 24580
  272.7 12.6 %all-to-all-start.2 = ((bf16[8,2,8192]{2,1,0:T(2,128)(2,1)}), bf16[8,2,8192]{2,1,0:T(2,128)(2,1)S(1)}, u32[]{:S(2)}, u32[]{:S(2)}) async-start(bf16[8,2,8192]{2,1,0:T(2,128)(2,1)} %reshape.311), calls=%async_computation.2 | async-start | bytes 524288 | tf_op jit(solution)/shard_map/all_to_all | solution.py:159
  357.6 27.3 %all-to-all-start.3 = ((bf16[1,128,3,16,64]{1,4,2,0,3:T(8,128)(2,1)}), bf16[1,128,3,16,64]{1,4,2,0,3:T(8,128)(2,1)S(1)}, u32[]{:S(2)}, u32[]{:S(2)}) async-start(bf16[1,128,3,16,64]{1,4,2,0,3:T(8,128)(2,1)} %copy.56), calls=%async_computation.3 | async-start | bytes 1572864 | tf_op jit(solution)/shard_map/all_to_all | solution.py:170
  399.9 23.5 %all-to-all-start.4 = ((bf16[8,1,128,2,64]{2,4,3,1,0:T(8,128)(2,1)}), bf16[8,1,128,2,64]{2,4,3,1,0:T(8,128)(2,1)S(1)}, u32[]{:S(2)}, u32[]{:S(2)}) async-start(bf16[8,1,128,2,64]{2,4,3,1,0:T(8,128)(2,1)} %constant_dynamic-update-slice_fusion), calls=%async_computation.4 | async-start | bytes 524288 | tf_op jit(solution)/shard_map/all_to_all | solution.py:173
  460.7 15.7 %copy-start = (bf16[2,1024,1024]{2,1,0:T(8,128)(2,1)S(1)}, bf16[2,1024,1024]{2,1,0:T(8,128)(2,1)}, u32[]{:S(2)}) copy-start(bf16[2,1024,1024]{2,1,0:T(8,128)(2,1)} %all-gather.17.cloned.1.call-done) | copy-start | bytes 12582916
Sparse Core Ops, SparseCore 0:
  10.2 58.9 all-gather.8
  72.0 60.5 all-gather.6
  135.5 55.0 all-gather.10
  193.4 61.0 all-gather.12
  257.3 95.1 all-gather.14
  355.3 68.0 all-gather.16
